TPU v7x, 16 devices: a whole 2x2x2 slice. The times are simulated.
16 devices in a mesh: rep: 1, dp: 16 (over x, y, z, core).
Axes of the slice: x: 2, y: 2, z: 2, core: 2. Of those that a mesh axis runs over, the one named last changes fastest.
Arguments:
- g_w_gate: bfloat16 [16, 2, 1280, 3584], P(('rep', 'dp'))
- g_w_up: bfloat16 [16, 2, 1280, 3584], P(('rep', 'dp'))
- g_w_down: bfloat16 [16, 2, 3584, 1280], P(('rep', 'dp'))
- w_gate: bfloat16 [2, 1280, 3584], replicated
- w_up: bfloat16 [2, 1280, 3584], replicated
- w_down: bfloat16 [2, 3584, 1280], replicated
- m_w_gate: float32 [2, 1280, 3584], P(None, 'dp')
- m_w_up: float32 [2, 1280, 3584], P(None, 'dp')
- m_w_down: float32 [2, 3584, 1280], P(None, 'dp')
- v_w_gate: float32 [2, 1280, 3584], P(None, 'dp')
- v_w_up: float32 [2, 1280, 3584], P(None, 'dp')
- v_w_down: float32 [2, 3584, 1280], P(None, 'dp')
Outputs:
- output 1: bfloat16 [2, 1280, 3584], P('rep')
- output 2: bfloat16 [2, 1280, 3584], P('rep')
- output 3: bfloat16 [2, 3584, 1280], P('rep')
- output 4: float32 [2, 1280, 3584], P('rep', 'dp')
- output 5: float32 [2, 1280, 3584], P('rep', 'dp')
- output 6: float32 [2, 3584, 1280], P('rep', 'dp')
- output 7: float32 [2, 1280, 3584], P('rep', 'dp')
- output 8: float32 [2, 1280, 3584], P('rep', 'dp')
- output 9: float32 [2, 3584, 1280], P('rep', 'dp')
All inputs are finite; a program needn't handle non-finite values.
Results may differ from a plain program's by a relative error of at most 0.022.
Values are sent between devices in bfloat16 or wider.
A program may use at most 2 GiB of HBM per device.

v0:
```python
import jax
import jax.numpy as jnp
from jax import lax
from jax.sharding import PartitionSpec as P


def adamw(w, m, v, g):
    m = 0.9 * m + 0.1 * g
    v = 0.95 * v + 0.05 * g * g
    step = m * lax.rsqrt(v + 1e-8) + 0.1 * w
    return (w - 0.02 * step).astype(jnp.bfloat16), m, v


def clipped(gradients, sum_of_squares, count):
    factor = jnp.minimum(1.0, 0.5 * lax.rsqrt(sum_of_squares / count + 1e-30))
    return [g * factor for g in gradients]


def solution(mesh):
    def step(*arrays):
        terms, weights, m, v = (arrays[i : i + 3] for i in (0, 3, 6, 9))
        gradients = [lax.psum_scatter(t[0], "dp", scatter_dimension=1, tiled=True).astype(jnp.float32) for t in terms]
        squares = lax.psum(sum(jnp.sum(g * g) for g in gradients), "dp")
        gradients = clipped(gradients, squares, lax.psum(1, "dp") * sum(g.size for g in gradients))
        me = lax.axis_index("dp")
        own = [lax.dynamic_slice_in_dim(w, me * one.shape[1], one.shape[1], 1).astype(jnp.float32) for w, one in zip(weights, m, strict=True)]
        new = [adamw(w, m, v, g) for w, m, v, g in zip(own, m, v, gradients, strict=True)]
        whole = [lax.all_gather(one[0], "dp", axis=1, tiled=True) for one in new]
        return (*whole, *(one[1] for one in new), *(one[2] for one in new))

    all_of, cut = P(None, None, None), P(None, "dp", None)
    return jax.shard_map(
        step,
        mesh=mesh,
        in_specs=(P(("rep", "dp"), None, None, None),) * 3 + (all_of,) * 3 + (cut,) * 6,
        out_specs=(P("rep", None, None),) * 3 + (P("rep", "dp", None),) * 6,
        check_vma=False,
    )
```

profile of v0, /device:TPU:0, one launch (start us, length us, event | category | flops | bytes accessed | tf_op | source)
XLA Modules:
  0.0 928.8 jit_solution(11454541455282494492)
XLA Ops:
  7.2 0.7 reduce-scatter.4.cloned.1.call-update
  8.0 0.7 reduce-scatter.6.cloned.1.call-update
  8.7 0.7 reduce-scatter.8.cloned.1.call-update
  9.4 0.0 all-gather.8.cloned.1.call-start
  9.5 191.2 %reduce-scatter.4.cloned.1.call-done = bf16[2,80,3584]{2,1,0:T(8,128)(2,1)} async-done(((bf16[2,1280,3584]{2,1,0:T(8,128)(2,1)}), bf16[2,80,3584]{2,1,0:T(8,128)(2,1)}) %reduce-scatter.4.cloned.1.call-update) | async-done | bytes 1146896 | tf_op jit(solution)/shard_map/reduce_scatter | solution.py:22
  200.6 2.5 fusion.9
  203.1 191.9 %reduce-scatter.6.cloned.1.call-done = bf16[2,80,3584]{2,1,0:T(8,128)(2,1)} async-done(((bf16[2,1280,3584]{2,1,0:T(8,128)(2,1)}), bf16[2,80,3584]{2,1,0:T(8,128)(2,1)}) %reduce-scatter.6.cloned.1.call-update) | async-done | bytes 1146896 | tf_op jit(solution)/shard_map/reduce_scatter | solution.py:22
  395.0 2.5 fusion.10
  398.7 190.5 %reduce-scatter.8.cloned.1.call-done = bf16[2,224,1280]{2,1,0:T(8,128)(2,1)} async-done(((bf16[2,3584,1280]{2,1,0:T(8,128)(2,1)}), bf16[2,224,1280]{2,1,0:T(8,128)(2,1)}) %reduce-scatter.8.cloned.1.call-update) | async-done | bytes 1146896 | tf_op jit(solution)/shard_map/reduce_scatter | solution.py:22
  589.2 2.5 fusion.11
  592.4 36.3 %psum.7 = f32[]{:T(128)} all-reduce(f32[]{:T(128)S(6)} %add.65), channel_id=1, replica_groups=mesh['rep'=1,'dp'=16] {'dp'}, use_global_device_ids=true, to_apply=%region_6.0 | all-reduce | flops 1 | bytes 8 | tf_op jit(solution)/shard_map/psum | solution.py:23
  629.4 5.6 fusion.17
  635.0 0.0 all-gather.4.cloned.1.call-start
  635.1 6.0 fusion.8
  641.1 0.0 all-gather.6.cloned.1.call-start
  641.1 5.9 fusion.14
  647.1 70.1 %all-gather.8.cloned.1.call-done = bf16[2,3584,1280]{2,1,0:T(8,128)(2,1)} async-done(((bf16[2,224,1280]{2,1,0:T(8,128)(2,1)}), bf16[2,3584,1280]{2,1,0:T(8,128)(2,1)}) %all-gather.8.cloned.1.call-update) | async-done | bytes 18350096 | tf_op jit(solution)/shard_map/all_gather | solution.py:28
  717.1 83.9 %all-gather.4.cloned.1.call-done = bf16[2,1280,3584]{2,1,0:T(8,128)(2,1)} async-done(((bf16[2,80,3584]{2,1,0:T(8,128)(2,1)}), bf16[2,1280,3584]{2,1,0:T(8,128)(2,1)}) %all-gather.4.cloned.1.call-update) | async-done | bytes 18350096 | tf_op jit(solution)/shard_map/all_gather | solution.py:28
  801.0 83.9 %all-gather.6.cloned.1.call-done = bf16[2,1280,3584]{2,1,0:T(8,128)(2,1)} async-done(((bf16[2,80,3584]{2,1,0:T(8,128)(2,1)}), bf16[2,1280,3584]{2,1,0:T(8,128)(2,1)}) %all-gather.6.cloned.1.call-update) | async-done | bytes 18350096 | tf_op jit(solution)/shard_map/all_gather | solution.py:28
  884.9 19.7 %copy.24 = bf16[2,1280,3584]{2,1,0:T(8,128)(2,1)} copy(bf16[2,1280,3584]{2,1,0:T(8,128)(2,1)} %all-gather.4.cloned.1.call-done) | data formatting | bytes 36700160
  904.6 9.3 %copy.25 = bf16[2,1280,3584]{2,1,0:T(8,128)(2,1)} copy(bf16[2,1280,3584]{2,1,0:T(8,128)(2,1)S(1)} %copy-done) | data formatting | bytes 36700160
  913.9 0.5 slice-done.3
  914.4 0.9 slice-done.4
  915.3 6.7 copy.26
  (23 shorter events, 0.2 us)
Async XLA Ops:
  7.2 193.5 %reduce-scatter.4.cloned.1.call-start = ((), (), s32[]{:S(2)}) async-start(), calls=%async_computation.3 | async-start | bytes 19496960 | tf_op jit(solution)/shard_map/reduce_scatter | solution.py:22
  7.9 387.1 %reduce-scatter.6.cloned.1.call-start = ((), (), s32[]{:S(2)}) async-start(), calls=%async_computation.4 | async-start | bytes 19496960 | tf_op jit(solution)/shard_map/reduce_scatter | solution.py:22
  8.7 580.6 %reduce-scatter.8.cloned.1.call-start = ((), (), s32[]{:S(2)}) async-start(), calls=%async_computation.5 | async-start | bytes 19496960 | tf_op jit(solution)/shard_map/reduce_scatter | solution.py:22
  9.4 620.0 %copy-start.3 = (f32[2,224,1280]{2,1,0:T(8,128)S(1)}, f32[2,224,1280]{2,1,0:T(8,128)}, u32[]{:S(2)}) copy-start(f32[2,224,1280]{2,1,0:T(8,128)} %param.23) | copy-start | bytes 6881284
  9.4 707.7 %all-gather.8.cloned.1.call-start = ((), (), s32[]{:S(2)}) async-start(), calls=%async_computation.8 | async-start | bytes 19496960 | tf_op jit(solution)/shard_map/all_gather | solution.py:28
  629.4 5.7 copy-start.2
  635.0 166.0 %all-gather.4.cloned.1.call-start = ((), (), s32[]{:S(2)}) async-start(), calls=%async_computation.6 | async-start | bytes 19496960 | tf_op jit(solution)/shard_map/all_gather | solution.py:28
  635.1 6.1 copy-start.1
  641.1 243.8 %all-gather.6.cloned.1.call-start = ((), (), s32[]{:S(2)}) async-start(), calls=%async_computation.7 | async-start | bytes 19496960 | tf_op jit(solution)/shard_map/all_gather | solution.py:28
  884.9 19.7 %copy-start = (bf16[2,1280,3584]{2,1,0:T(8,128)(2,1)S(1)}, bf16[2,1280,3584]{2,1,0:T(8,128)(2,1)}, u32[]{:S(2)}) copy-start(bf16[2,1280,3584]{2,1,0:T(8,128)(2,1)} %all-gather.6.cloned.1.call-done) | copy-start | bytes 55050244
  884.9 29.0 %slice-start = ((s8[18350080]{0:T(1024)(128)(4,1)}), s8[4194304]{0:T(1024)(128)(4,1)S(1)}, s32[]{:S(2)}) async-start(s8[18350080]{0:T(1024)(128)(4,1)} %bitcast.6), calls=%async_computation.9 | async-start | bytes 8388608
  884.9 29.0 %slice-start.1 = ((s8[18350080]{0:T(1024)(128)(4,1)}), s8[4194304]{0:T(1024)(128)(4,1)S(1)}, s32[]{:S(2)}) async-start(s8[18350080]{0:T(1024)(128)(4,1)} %bitcast.6), calls=%async_computation.10 | async-start | bytes 8388608
  884.9 29.0 %slice-start.2 = ((s8[18350080]{0:T(1024)(128)(4,1)}), s8[4194304]{0:T(1024)(128)(4,1)S(1)}, s32[]{:S(2)}) async-start(s8[18350080]{0:T(1024)(128)(4,1)} %bitcast.6), calls=%async_computation.11 | async-start | bytes 8388608
  904.6 9.8 %slice-start.3 = ((s8[18350080]{0:T(1024)(128)(4,1)}), s8[4194304]{0:T(1024)(128)(4,1)S(1)}, s32[]{:S(2)}) async-start(s8[18350080]{0:T(1024)(128)(4,1)} %bitcast.6), calls=%async_computation.12 | async-start | bytes 8388608
  904.6 10.7 %slice-start.4 = ((s8[18350080]{0:T(1024)(128)(4,1)}), s8[1572864]{0:T(1024)(128)(4,1)S(1)}, s32[]{:S(2)}) async-start(s8[18350080]{0:T(1024)(128)(4,1)} %bitcast.6), calls=%async_computation.13 | async-start | bytes 3145728
Sparse Core Ops, SparseCore 0:
  10.3 190.3 reduce-scatter.3
  202.9 191.9 reduce-scatter.5
  397.3 191.9 reduce-scatter.7
  635.1 81.9 all-gather.7
  719.8 81.1 all-gather.3
  803.7 81.1 all-gather.5
where the time goes:
time: 929 us
  waiting for transfers between devices  814 us (88%)
  local copies, waits for them, and re-layouts  37.1 us (4%)
  blocking collectives  36.3 us (4%)
  other arithmetic  24.8 us (3%)
  between operations  16.8 us (2%)
    reduce_scatter x3, waiting for transfers between devices, step(): lax.psum_scatter(t[0], 'dp', scatter_dimension=1, tiled=True)  574 us
    all_gather x3, waiting for transfers between devices, step(): whole = [lax.all_gather(one[0], 'dp', axis=1, tiled=True) for one in new]  238 us
    unnamed x21, local copies, waits for them, and re-layouts  37.1 us
    psum x1, blocking collectives, step(): squares = lax.psum(sum((jnp.sum(g * g) for g in gradients)), 'dp')  36.3 us
  transfers between devices with their start and end apart: 6, of which 6 were waited for; matrix products, arithmetic and copies ran while one was open for 2% of the time, Pallas kernels for 0%

commit v1 on v0

v1 whole, which is shorter than its diff:
```python
import jax
import jax.numpy as jnp
from jax import lax
from jax.experimental import pallas as pl
from jax.experimental.pallas import tpu as pltpu
from jax.sharding import PartitionSpec as P

MESH = pl.DeviceIdType.MESH
F32, BF16 = jnp.float32, jnp.bfloat16
LAYERS = 2
PARTS = 14
WAVES = LAYERS * PARTS
SLOTS = 8
AHEAD = 3
ORDERS = ((0, 1, 2), (1, 2, 0), (2, 0, 1))
BITS = (8, 4, 2)


def flip(me, bit):
    return me + bit * (1 - 2 * ((me // bit) % 2))


class Weight:
    def __init__(self, k, rows, columns):
        self.k, self.rows, self.columns = k, rows, columns
        self.by_columns = columns > rows * 8
        self.shape = (rows, columns // PARTS) if self.by_columns else (rows // PARTS, columns)
        self.axes = ORDERS[k]
        self.rest = tuple(sorted(self.axes[1:]))

    def part(self, wave):
        layer, cut = wave // PARTS, wave % PARTS
        if self.by_columns:
            wide = self.shape[1]
            return layer, (slice(None), pl.ds(pl.multiple_of(cut * wide, wide), wide))
        tall = self.shape[0]
        return layer, (pl.ds(pl.multiple_of(cut * tall, tall), tall), slice(None))


def where(fixed):
    return tuple(fixed.get(axis, slice(None)) for axis in range(3))


def kernel(weights, count, *refs):
    it = iter(refs)
    take = lambda: [next(it) for _ in weights]
    g_in, w_in, m_in, v_in = take(), take(), take(), take()
    w_out, m_out, v_out = take(), take(), take()
    own, other, first, second, third = take(), take(), take(), take(), take()
    g_own, w_own, m_own, v_own, squares = take(), take(), take(), take(), take()
    part_sum, all_sums = next(it), next(it)
    (load_sem, die_send, die_recv, send_sem, recv_sem, gather_send, gather_recv, back_send, back_recv, local_sem, state_sem, sum_send, sum_recv, credit) = it

    me = lax.axis_index("dp")
    core = me % 2
    at = tuple((me // bit) % 2 for bit in BITS)
    near = tuple(flip(me, bit) for bit in BITS)
    twin = flip(me, 1)

    def remote(src, dst, send, recv, device):
        return pltpu.make_async_remote_copy(src_ref=src, dst_ref=dst, send_sem=send, recv_sem=recv, device_id={"dp": device}, device_id_type=MESH)

    def load(w, wave):
        layer, cut = w.part(wave)
        slot = wave % SLOTS
        return pltpu.make_async_copy(g_in[w.k].at[(layer, slice(None), slice(None), slice(None), core, *cut)], own[w.k].at[slot], load_sem.at[slot, w.k])

    def swap(w, wave):
        layer, cut = w.part(wave)
        slot = wave % SLOTS
        src = g_in[w.k].at[(layer, slice(None), slice(None), slice(None), 1 - core, *cut)]
        return remote(src, other[w.k].at[slot], die_send.at[slot, w.k], die_recv.at[slot, w.k], twin)

    def away(w, stage):
        fixed = {axis: at[axis] for axis in w.axes[:stage]}
        fixed[w.axes[stage]] = 1 - at[w.axes[stage]]
        return fixed

    def pass_on(w, wave, stage):
        slot = wave % SLOTS
        src = own[w.k].at[(slot, *where(away(w, stage)))]
        dst = (first, second, third)[stage][w.k].at[slot]
        return remote(src, dst, send_sem.at[slot, stage, w.k], recv_sem.at[slot, stage, w.k], near[w.axes[stage]])

    def total(w, slot, block, stage):
        so_far = own[w.k][(slot, *block)].astype(F32) + other[w.k][(slot, *block)].astype(F32)
        if stage > 0:
            so_far += first[w.k][(slot, *(block[axis] for axis in w.rest))].astype(F32)
        if stage > 1:
            so_far += second[w.k][slot, block[w.axes[2]]].astype(F32)
        if stage > 2:
            so_far += third[w.k][slot].astype(F32)
        return so_far

    def sum_and_pass(w, wave, stage):
        slot = wave % SLOTS
        fixed = away(w, stage)
        free = [axis for axis in range(3) if axis not in fixed]

        @pl.loop(0, 2 ** len(free))
        def _(i):
            block = dict(fixed)
            for n, axis in enumerate(free):
                block[axis] = (i // 2**n) % 2
            block = tuple(block[axis] for axis in range(3))
            own[w.k][(slot, *block)] = total(w, slot, block, stage).astype(BF16)

        pass_on(w, wave, stage).start()

    def finish(w, wave):
        layer, cut = w.part(wave)
        g = total(w, wave % SLOTS, at, 3).astype(BF16)
        g_own[w.k][(layer, *cut)] = g
        g = g.astype(F32)
        g = g * g
        squares[w.k][...] += sum(g[8 * i : 8 * i + 8] for i in range(w.shape[0] // 8))

    def state_copies():
        copies = []
        for w in weights:
            copies += [
                pltpu.make_async_copy(m_in[w.k], m_own[w.k], state_sem.at[0, w.k]),
                pltpu.make_async_copy(v_in[w.k], v_own[w.k], state_sem.at[1, w.k]),
                pltpu.make_async_copy(w_in[w.k].at[(slice(None), *at, core)], w_own[w.k], state_sem.at[2, w.k]),
            ]
        return copies

    def state_out():
        copies = []
        for w in weights:
            copies += [
                pltpu.make_async_copy(m_own[w.k], m_out[w.k], state_sem.at[3, w.k]),
                pltpu.make_async_copy(v_own[w.k], v_out[w.k], state_sem.at[4, w.k]),
            ]
        return copies

    for w in weights:
        for wave in range(AHEAD):
            load(w, wave).start()
    for w in weights:
        squares[w.k][...] = jnp.zeros_like(squares[w.k])

    barrier = pltpu.get_barrier_semaphore()
    for k in range(1, 16):
        pl.semaphore_signal(barrier, inc=1, device_id={"dp": (me + k) % 16}, device_id_type=MESH)
    pl.semaphore_wait(barrier, 15)

    for wave in range(AHEAD):
        for w in weights:
            swap(w, wave).start()
    for copy in state_copies():
        copy.start()

    def drain(wave):
        for w in weights:
            swap(w, wave).wait_send()
            for stage in range(3):
                pass_on(w, wave, stage).wait_send()

    @pl.loop(0, WAVES + 3)
    def _(step):
        @pl.when(step < WAVES)
        def _():
            for w in weights:
                load(w, step).wait()
                swap(w, step).wait_recv()
                sum_and_pass(w, step, 0)

        @pl.when(step + AHEAD < WAVES)
        def _():
            wave = step + AHEAD

            @pl.when(wave >= SLOTS)
            def _():
                drain(wave - SLOTS)
                pl.semaphore_wait(credit, 1)

            for w in weights:
                load(w, wave).start()
                swap(w, wave).start()

        for stage in (1, 2):

            @pl.when((step >= stage) & (step - stage < WAVES))
            def _():
                for w in weights:
                    pass_on(w, step - stage, stage - 1).wait_recv()
                    sum_and_pass(w, step - stage, stage)

        @pl.when(step >= 3)
        def _():
            for w in weights:
                pass_on(w, step - 3, 2).wait_recv()
                finish(w, step - 3)

            @pl.when(step - 3 + SLOTS < WAVES)
            def _():
                pl.semaphore_signal(credit, inc=1, device_id={"dp": twin}, device_id_type=MESH)

    @pl.loop(WAVES - SLOTS, WAVES)
    def _(wave):
        drain(wave)

    mine = jnp.zeros((8, 128), F32)
    for w in weights:
        for i in range(w.shape[1] // 128):
            mine += squares[w.k][:, 128 * i : 128 * i + 128]
    part_sum[...] = mine

    def tell(k):
        return remote(part_sum, all_sums.at[k - 1], sum_send.at[k - 1], sum_recv.at[k - 1], (me + k) % 16)

    for k in range(1, 16):
        tell(k).start()
    for copy in state_copies():
        copy.wait()
    sums = mine
    for k in range(1, 16):
        tell(k).wait_recv()
        sums += all_sums[k - 1]
    sums = jnp.sum(jnp.sum(sums, axis=0, keepdims=True), axis=1, keepdims=True)
    factor = jnp.minimum(1.0, 0.5 * lax.rsqrt(sums / count + 1e-30))

    def update(w, wave):
        layer, cut = w.part(wave)
        here = (layer, *cut)
        g = g_own[w.k][here].astype(F32) * factor
        m = 0.9 * m_own[w.k][here] + 0.1 * g
        v = 0.95 * v_own[w.k][here] + 0.05 * g * g
        weight = w_own[w.k][here].astype(F32)
        w_own[w.k][here] = (weight - 0.02 * (m * lax.rsqrt(v + 1e-8) + 0.1 * weight)).astype(BF16)
        m_own[w.k][here] = m
        v_own[w.k][here] = v

    def out_at(w, wave, fixed, which):
        layer, cut = w.part(wave)
        return w_out[w.k].at[(layer, *where(fixed), which, *cut)]

    def keep(w, wave):
        layer, cut = w.part(wave)
        return pltpu.make_async_copy(w_own[w.k].at[(layer, *cut)], out_at(w, wave, dict(enumerate(at)), core), local_sem.at[wave % SLOTS, w.k])

    def give(w, wave, stage):
        slot = wave % SLOTS
        axes = w.axes[::-1]
        dst = out_at(w, wave, {axis: at[axis] for axis in axes[stage:]}, core)
        layer, cut = w.part(wave)
        src = w_own[w.k].at[(layer, *cut)] if stage == 0 else dst
        return remote(src, dst, gather_send.at[slot, stage, w.k], gather_recv.at[slot, stage, w.k], near[axes[stage]])

    def give_twin(w, wave, half):
        slot = wave % SLOTS
        axis = w.axes[0]
        side = at[axis] if half == 0 else 1 - at[axis]
        ref = out_at(w, wave, {axis: side}, core)
        return remote(ref, ref, back_send.at[slot, half, w.k], back_recv.at[slot, half, w.k], twin)

    @pl.loop(0, WAVES + 7)
    def _(step):
        @pl.when(step < WAVES)
        def _():
            for w in weights:
                update(w, step)
                give(w, step, 0).start()
                keep(w, step).start()

        @pl.when((step >= 1) & (step - 1 < WAVES))
        def _():
            for w in weights:
                keep(w, step - 1).wait()
                give(w, step - 1, 0).wait_recv()
                give(w, step - 1, 1).start()

        @pl.when((step >= 2) & (step - 2 < WAVES))
        def _():
            for w in weights:
                give(w, step - 2, 1).wait_recv()
                give(w, step - 2, 2).start()
                give_twin(w, step - 2, 0).start()

        @pl.when((step >= 3) & (step - 3 < WAVES))
        def _():
            for w in weights:
                give(w, step - 3, 2).wait_recv()
                give_twin(w, step - 3, 1).start()

        @pl.when((step >= 5) & (step - 5 < WAVES))
        def _():
            for w in weights:
                for half in range(2):
                    give_twin(w, step - 5, half).wait_recv()

        @pl.when((step >= 7) & (step - 7 < WAVES))
        def _():
            for w in weights:
                for stage in range(3):
                    give(w, step - 7, stage).wait_send()
                for half in range(2):
                    give_twin(w, step - 7, half).wait_send()

        @pl.when(step == WAVES)
        def _():
            for copy in state_out():
                copy.start()

    for copy in state_out():
        copy.wait()
    for k in range(1, 16):
        tell(k).wait_send()


def solution(mesh):
    def step(*arrays):
        terms, whole, m, v = (arrays[i : i + 3] for i in (0, 3, 6, 9))
        weights = [Weight(k, *one.shape[1:]) for k, one in enumerate(m)]
        count = 16 * sum(one.size for one in m)
        cut = [(LAYERS, 2, 2, 2, 2, w.rows, w.columns) for w in weights]
        held = lambda n, extra=(): [pltpu.VMEM((n, *extra, *w.shape), BF16) for w in weights]
        block = lambda dtype: [pltpu.VMEM((LAYERS, w.rows, w.columns), dtype) for w in weights]
        scratch = (
            held(SLOTS, (2, 2, 2))
            + held(SLOTS, (2, 2, 2))
            + held(SLOTS, (2, 2))
            + held(SLOTS, (2,))
            + held(SLOTS)
            + block(BF16)
            + block(BF16)
            + block(F32)
            + block(F32)
            + [pltpu.VMEM((8, w.shape[1]), F32) for w in weights]
            + [pltpu.VMEM((8, 128), F32), pltpu.VMEM((15, 8, 128), F32)]
            + [pltpu.SemaphoreType.DMA((SLOTS, 3))] * 3
            + [pltpu.SemaphoreType.DMA((SLOTS, 3, 3))] * 4
            + [pltpu.SemaphoreType.DMA((SLOTS, 2, 3))] * 2
            + [pltpu.SemaphoreType.DMA((SLOTS, 3)), pltpu.SemaphoreType.DMA((5, 3))]
            + [pltpu.SemaphoreType.DMA((15,))] * 2
            + [pltpu.SemaphoreType.REGULAR]
        )
        anywhere = pl.BlockSpec(memory_space=pl.ANY)
        out = pl.pallas_call(
            lambda *refs: kernel(weights, float(count), *refs),
            out_shape=[jax.ShapeDtypeStruct(c, BF16) for c in cut] + [jax.ShapeDtypeStruct(one.shape, F32) for one in (*m, *v)],
            in_specs=[anywhere] * 12,
            out_specs=[anywhere] * 9,
            scratch_shapes=scratch,
            compiler_params=pltpu.CompilerParams(collective_id=0, has_side_effects=True, vmem_limit_bytes=60 * 2**20),
            name="step",
        )(*(t.reshape(c) for t, c in zip(terms, cut)), *(t.reshape(c) for t, c in zip(whole, cut)), *m, *v)
        return (*(o.reshape(t.shape) for o, t in zip(out[:3], whole)), *out[3:])

    all_of, cut = P(None, None, None), P(None, "dp", None)
    return jax.shard_map(
        step,
        mesh=mesh,
        in_specs=(P(("rep", "dp"), None, None, None),) * 3 + (all_of,) * 3 + (cut,) * 6,
        out_specs=(P("rep", None, None),) * 3 + (P("rep", "dp", None),) * 6,
        check_vma=False,
    )
```

time: 929 us -> 420 us (0.45)
  waiting for transfers between devices: 814 us -> 0 us
  Pallas kernels: 0 us -> 368 us
  blocking collectives: 36.3 us -> 0 us
  other arithmetic: 24.8 us -> 0.01 us
  between operations: 16.8 us -> 0.7 us
  local copies, waits for them, and re-layouts: 37.1 us -> 51 us
    reduce_scatter x3 -> x0, waiting for transfers between devices: 574 us -> none  [step(): lax.psum_scatter(t[0], 'dp', scatter_dimension=1, tiled=True)]
    pallas_call x0 -> x1, Pallas kernels: none -> 368 us  [step(): pl.pallas_call(lambda *refs: kernel(weights, float(count), *refs), out_sh...]
    all_gather x3 -> x0, waiting for transfers between devices: 238 us -> none  [step(): whole = [lax.all_gather(one[0], 'dp', axis=1, tiled=True) for one in new]]
    psum x1 -> x0, blocking collectives: 36.3 us -> none  [step(): squares = lax.psum(sum((jnp.sum(g * g) for g in gradients)), 'dp')]
    convert_element_type x3 -> x0, other arithmetic: 17.5 us -> none  [adamw(): return ((w - 0.02 * step).astype(jnp.bfloat16), m, v)]
    unnamed x21 -> x33, local copies, waits for them, and re-layouts: 37.1 us -> 51 us
  transfers between devices with their start and end apart: 6 -> 0, of which waited for: 6 -> 0; matrix products, arithmetic and copies ran while one was open for 2% -> 0% of each run, Pallas kernels for 0% -> 0%
where the time goes in v1:
time: 420 us
  Pallas kernels  368 us (88%)
  local copies, waits for them, and re-layouts  51 us (12%)
    pallas_call x1, Pallas kernels, step(): pl.pallas_call(lambda *refs: kernel(weights, float(count), *refs), out_sh...  368 us
    unnamed x33, local copies, waits for them, and re-layouts  51 us

profile of v1, /device:TPU:0, one launch (start us, length us, event | category | flops | bytes accessed | tf_op | source)
XLA Modules:
  0.0 420.0 jit_solution(18112823687117497620)
XLA Ops:
  0.6 368.3 %step.1 = (bf16[2,2,2,2,2,80,3584]{6,5,4,3,2,1,0:T(8,128)(2,1)}, bf16[2,2,2,2,2,80,3584]{6,5,4,3,2,1,0:T(8,128)(2,1)}, bf16[2,2,2,2,2,224,1280]{6,5,4,3,2,1,0:T(...) custom-call(bf16[2,2,2,2,2,80,3584]{6,5,4,3,2,1,0:T(8,128)(2,1)} %bi, ...), custom_call_target="tpu_custom_call" | custom-call | tf_op jit(solution)/shard_map/step/pallas_call | solution.py:340
  369.0 0.0 copy-start
  369.0 0.0 slice-start
  369.0 0.0 slice-start.1
  369.0 0.0 slice-start.2
  369.0 19.7 %copy.30 = bf16[2,1280,3584]{2,1,0:T(8,128)(2,1)} copy(bf16[2,1280,3584]{2,1,0:T(8,128)(2,1)} %bitcast.13) | data formatting | bytes 36700160
  388.7 0.0 copy-done
  388.7 9.3 %copy.31 = bf16[2,1280,3584]{2,1,0:T(8,128)(2,1)} copy(bf16[2,1280,3584]{2,1,0:T(8,128)(2,1)S(1)} %bitcast.12) | data formatting | bytes 36700160
  398.0 0.0 slice-done
  398.0 0.0 slice-done.2
  398.0 0.3 slice-done.3
  398.4 1.0 slice-done.4
  399.4 6.9 %copy.32 = bf16[2,3584,1280]{2,1,0:T(8,128)(2,1)} copy(bf16[2,3584,1280]{2,1,0:T(8,128)(2,1)S(1)} %bitcast.11) | data formatting | bytes 36700160
  406.3 1.4 copy.33
  407.7 1.1 copy-done.5
  408.8 1.4 copy.34
  410.1 1.1 copy-done.4
  411.2 1.4 copy.35
  412.6 1.1 copy-done.3
  413.7 1.4 copy.36
  415.1 1.1 copy-done.2
  416.2 1.4 copy.37
  417.6 1.1 copy-done.1
  418.7 1.4 copy.38
  (11 shorter events, 0.0 us)
Async XLA Ops:
  369.0 19.7 %copy-start = (bf16[2,2,2,2,2,80,3584]{6,5,4,3,2,1,0:T(8,128)(2,1)S(1)}, bf16[2,2,2,2,2,80,3584]{6,5,4,3,2,1,0:T(8,128)(2,1)}, u32[]{:S(2)}) copy-start(bf16[2,2,2,2,2,80,3584]{6,5,4,3,2,1,0:T(8,128)(2,1)} %get-tuple-element.19) | copy-start | bytes 55050244
  369.0 29.0 %slice-start = ((s8[18350080]{0:T(1024)(128)(4,1)}), s8[4194304]{0:T(1024)(128)(4,1)S(1)}, s32[]{:S(2)}) async-start(s8[18350080]{0:T(1024)(128)(4,1)} %bitcast.9), calls=%async_computation | async-start | bytes 8388608
  369.0 29.0 %slice-start.1 = ((s8[18350080]{0:T(1024)(128)(4,1)}), s8[4194304]{0:T(1024)(128)(4,1)S(1)}, s32[]{:S(2)}) async-start(s8[18350080]{0:T(1024)(128)(4,1)} %bitcast.9), calls=%async_computation.1 | async-start | bytes 8388608
  369.0 29.0 %slice-start.2 = ((s8[18350080]{0:T(1024)(128)(4,1)}), s8[4194304]{0:T(1024)(128)(4,1)S(1)}, s32[]{:S(2)}) async-start(s8[18350080]{0:T(1024)(128)(4,1)} %bitcast.9), calls=%async_computation.2 | async-start | bytes 8388608
  388.7 9.7 %slice-start.3 = ((s8[18350080]{0:T(1024)(128)(4,1)}), s8[4194304]{0:T(1024)(128)(4,1)S(1)}, s32[]{:S(2)}) async-start(s8[18350080]{0:T(1024)(128)(4,1)} %bitcast.9), calls=%async_computation.3 | async-start | bytes 8388608
  388.7 10.7 %slice-start.4 = ((s8[18350080]{0:T(1024)(128)(4,1)}), s8[1572864]{0:T(1024)(128)(4,1)S(1)}, s32[]{:S(2)}) async-start(s8[18350080]{0:T(1024)(128)(4,1)} %bitcast.9), calls=%async_computation.4 | async-start | bytes 3145728
  399.4 6.9 %copy-start.6 = (f32[2,80,3584]{2,1,0:T(8,128)S(1)}, f32[2,80,3584]{2,1,0:T(8,128)}, u32[]{:S(2)}) copy-start(f32[2,80,3584]{2,1,0:T(8,128)} %get-tuple-element.39) | copy-start | bytes 6881284
  406.3 2.5 copy-start.5
  408.8 2.5 copy-start.4
  411.2 2.5 copy-start.3
  413.7 2.5 copy-start.2
  416.2 2.5 copy-start.1

commit v2 on v1

v2 whole, which is shorter than its diff:
```python
import jax
import jax.numpy as jnp
from jax import lax
from jax.experimental import pallas as pl
from jax.experimental.pallas import tpu as pltpu
from jax.sharding import PartitionSpec as P

MESH = pl.DeviceIdType.MESH
F32, BF16 = jnp.float32, jnp.bfloat16
LAYERS = 2
PARTS = 14
WAVES = LAYERS * PARTS
SLOTS = 8
HELD = 6
RING = 4
ROOM = 32
GRANT = 8 * 2**20
AHEAD = 3
ORDERS = ((0, 1, 2), (1, 2, 0), (2, 0, 1))
BITS = (8, 4, 2)


def flip(me, bit):
    return me + bit * (1 - 2 * ((me // bit) % 2))


class Weight:
    def __init__(self, k, rows, columns):
        self.k, self.rows, self.columns = k, rows, columns
        self.by_columns = columns > rows * 8
        self.shape = (rows, columns // PARTS) if self.by_columns else (rows // PARTS, columns)
        self.axes = ORDERS[k]
        self.rest = tuple(sorted(self.axes[1:]))

    def part(self, wave):
        layer, cut = wave // PARTS, wave % PARTS
        if self.by_columns:
            wide = self.shape[1]
            return layer, (slice(None), pl.ds(pl.multiple_of(cut * wide, wide), wide))
        tall = self.shape[0]
        return layer, (pl.ds(pl.multiple_of(cut * tall, tall), tall), slice(None))


def where(fixed):
    return tuple(fixed.get(axis, slice(None)) for axis in range(3))


def kernel(weights, count, *refs):
    it = iter(refs)
    take = lambda: [next(it) for _ in weights]
    g_in, w_in, m_in, v_in = take(), take(), take(), take()
    w_out, state_out = take(), take()
    first, second, third = take(), take(), take()
    w_own, m_own, v_own, squares = take(), take(), take(), take()
    part_sum, all_sums = next(it), next(it)
    (load_sem, die_send, die_recv, send_sem, recv_sem, gather_send, gather_recv, back_send, back_recv, state_sem, sum_send, sum_recv) = it

    me = lax.axis_index("dp")
    core = me % 2
    at = tuple((me // bit) % 2 for bit in BITS)
    near = tuple(flip(me, bit) for bit in BITS)
    twin = flip(me, 1)

    def remote(src, dst, send, recv, device):
        return pltpu.make_async_remote_copy(src_ref=src, dst_ref=dst, send_sem=send, recv_sem=recv, device_id={"dp": device}, device_id_type=MESH)

    def load(w, wave):
        layer, cut = w.part(wave)
        spot = (layer, slice(None), slice(None), slice(None), core, *cut)
        return pltpu.make_async_copy(g_in[w.k].at[spot], w_out[w.k].at[spot], load_sem.at[wave % SLOTS, w.k])

    def swap(w, wave):
        layer, cut = w.part(wave)
        slot = wave % SLOTS
        src = g_in[w.k].at[(layer, slice(None), slice(None), slice(None), 1 - core, *cut)]
        dst = w_out[w.k].at[(layer, slice(None), slice(None), slice(None), core, *cut)]
        return remote(src, dst, die_send.at[slot, w.k], die_recv.at[slot, w.k], twin)

    def away(w, stage):
        fixed = {axis: at[axis] for axis in w.axes[:stage]}
        fixed[w.axes[stage]] = 1 - at[w.axes[stage]]
        return fixed

    def pass_on(w, wave, stage):
        layer, cut = w.part(wave)
        src = w_out[w.k].at[(layer, *where(away(w, stage)), core, *cut)]
        dst = (first, second, third)[stage][w.k].at[wave % HELD]
        send, recv = send_sem.at[wave % SLOTS, stage, w.k], recv_sem.at[wave % HELD, stage, w.k]
        return remote(src, dst, send, recv, near[w.axes[stage]])

    def total(w, wave, block, stage):
        layer, cut = w.part(wave)
        slot = wave % HELD
        so_far = w_out[w.k][(layer, *block, core, *cut)].astype(F32) + w_out[w.k][(layer, *block, 1 - core, *cut)].astype(F32)
        if stage > 0:
            so_far += first[w.k][(slot, *(block[axis] for axis in w.rest))].astype(F32)
        if stage > 1:
            so_far += second[w.k][slot, block[w.axes[2]]].astype(F32)
        if stage > 2:
            so_far += third[w.k][slot].astype(F32)
        return so_far

    def sum_and_pass(w, wave, stage):
        layer, cut = w.part(wave)
        fixed = away(w, stage)
        free = [axis for axis in range(3) if axis not in fixed]

        @pl.loop(0, 2 ** len(free))
        def _(i):
            block = dict(fixed)
            for n, axis in enumerate(free):
                block[axis] = (i // 2**n) % 2
            block = tuple(block[axis] for axis in range(3))
            w_out[w.k][(layer, *block, core, *cut)] = total(w, wave, block, stage).astype(BF16)

        pass_on(w, wave, stage).start()

    def finish(w, wave):
        layer, cut = w.part(wave)
        g = total(w, wave, at, 3).astype(BF16)
        w_out[w.k][(layer, *at, core, *cut)] = g
        g = g.astype(F32)
        g = g * g
        squares[w.k][...] += sum(g[8 * i : 8 * i + 8] for i in range(w.shape[0] // 8))

    def fetch(w, wave):
        layer, cut = w.part(wave)
        slot = wave % RING
        return (
            pltpu.make_async_copy(m_in[w.k].at[(layer, *cut)], m_own[w.k].at[slot], state_sem.at[slot, 0, w.k]),
            pltpu.make_async_copy(v_in[w.k].at[(layer, *cut)], v_own[w.k].at[slot], state_sem.at[slot, 1, w.k]),
            pltpu.make_async_copy(w_in[w.k].at[(layer, *at, core, *cut)], w_own[w.k].at[slot], state_sem.at[slot, 2, w.k]),
        )

    def put(w, wave):
        layer, cut = w.part(wave)
        slot = wave % RING
        return (
            pltpu.make_async_copy(m_own[w.k].at[slot], state_out[w.k].at[(0, layer, *cut)], state_sem.at[slot, 3, w.k]),
            pltpu.make_async_copy(v_own[w.k].at[slot], state_out[w.k].at[(1, layer, *cut)], state_sem.at[slot, 4, w.k]),
        )

    for wave in range(AHEAD):
        for w in weights:
            load(w, wave).start()
    for w in weights:
        squares[w.k][...] = jnp.zeros_like(squares[w.k])

    barrier = pltpu.get_barrier_semaphore()
    for k in range(1, 16):
        pl.semaphore_signal(barrier, inc=1, device_id={"dp": (me + k) % 16}, device_id_type=MESH)
    pl.semaphore_wait(barrier, 15)

    for wave in range(AHEAD):
        for w in weights:
            swap(w, wave).start()
    for wave in range(RING):
        for w in weights:
            for copy in fetch(w, wave):
                copy.start()

    def drain(wave):
        for w in weights:
            swap(w, wave).wait_send()
            for stage in range(3):
                pass_on(w, wave, stage).wait_send()

    @pl.loop(0, WAVES + 3)
    def _(step):
        @pl.when(step < WAVES)
        def _():
            for w in weights:
                load(w, step).wait()
                swap(w, step).wait_recv()
                sum_and_pass(w, step, 0)

        @pl.when(step + AHEAD < WAVES)
        def _():
            wave = step + AHEAD

            @pl.when(wave >= SLOTS)
            def _():
                drain(wave - SLOTS)

            for w in weights:
                load(w, wave).start()
                swap(w, wave).start()

        for stage in (1, 2):

            @pl.when((step >= stage) & (step - stage < WAVES))
            def _():
                for w in weights:
                    pass_on(w, step - stage, stage - 1).wait_recv()
                    sum_and_pass(w, step - stage, stage)

        @pl.when(step >= 3)
        def _():
            for w in weights:
                pass_on(w, step - 3, 2).wait_recv()
                finish(w, step - 3)

    @pl.loop(WAVES - SLOTS, WAVES)
    def _(wave):
        drain(wave)

    mine = jnp.zeros((8, 128), F32)
    for w in weights:
        for i in range(w.shape[1] // 128):
            mine += squares[w.k][:, 128 * i : 128 * i + 128]
    part_sum[...] = mine

    def tell(k):
        return remote(part_sum, all_sums.at[k - 1], sum_send.at[k - 1], sum_recv.at[k - 1], (me + k) % 16)

    for k in range(1, 16):
        tell(k).start()
    sums = mine
    for k in range(1, 16):
        tell(k).wait_recv()
        sums += all_sums[k - 1]
    sums = jnp.sum(jnp.sum(sums, axis=0, keepdims=True), axis=1, keepdims=True)
    factor = jnp.minimum(1.0, 0.5 * lax.rsqrt(sums / count + 1e-30))

    def update(w, wave):
        layer, cut = w.part(wave)
        here = (layer, *at, core, *cut)
        slot = wave % RING
        g = w_out[w.k][here].astype(F32) * factor
        m = 0.9 * m_own[w.k][slot] + 0.1 * g
        v = 0.95 * v_own[w.k][slot] + 0.05 * g * g
        weight = w_own[w.k][slot].astype(F32)
        w_out[w.k][here] = (weight - 0.02 * (m * lax.rsqrt(v + 1e-8) + 0.1 * weight)).astype(BF16)
        m_own[w.k][slot] = m
        v_own[w.k][slot] = v

    def out_at(w, wave, fixed, which):
        layer, cut = w.part(wave)
        return w_out[w.k].at[(layer, *where(fixed), which, *cut)]

    def give(w, wave, stage):
        slot = wave % SLOTS
        axes = w.axes[::-1]
        ref = out_at(w, wave, {axis: at[axis] for axis in axes[stage:]}, core)
        return remote(ref, ref, gather_send.at[slot, stage, w.k], gather_recv.at[slot, stage, w.k], near[axes[stage]])

    def give_twin(w, wave, half):
        slot = wave % SLOTS
        axis = w.axes[0]
        side = at[axis] if half == 0 else 1 - at[axis]
        ref = out_at(w, wave, {axis: side}, core)
        return remote(ref, ref, back_send.at[slot, half, w.k], back_recv.at[slot, half, w.k], twin)

    @pl.loop(0, WAVES + 7)
    def _(step):
        @pl.when(step < WAVES)
        def _():
            for w in weights:
                for copy in fetch(w, step):
                    copy.wait()
                update(w, step)
                give(w, step, 0).start()
                for copy in put(w, step):
                    copy.start()

        @pl.when((step >= 1) & (step - 1 < WAVES))
        def _():
            for w in weights:
                give(w, step - 1, 0).wait_recv()
                give(w, step - 1, 1).start()

        @pl.when((step >= 2) & (step - 2 < WAVES))
        def _():
            for w in weights:
                give(w, step - 2, 1).wait_recv()
                give(w, step - 2, 2).start()
                give_twin(w, step - 2, 0).start()

        @pl.when((step >= 3) & (step - 3 < WAVES))
        def _():
            for w in weights:
                give(w, step - 3, 2).wait_recv()
                give_twin(w, step - 3, 1).start()

        @pl.when((step >= 2) & (step - 2 < WAVES))
        def _():
            for w in weights:
                for copy in put(w, step - 2):
                    copy.wait()

        @pl.when((step >= 2) & (step + 2 < WAVES))
        def _():
            for w in weights:
                for copy in fetch(w, step + 2):
                    copy.start()

        @pl.when((step >= 5) & (step - 5 < WAVES))
        def _():
            for w in weights:
                for half in range(2):
                    give_twin(w, step - 5, half).wait_recv()

        @pl.when((step >= 7) & (step - 7 < WAVES))
        def _():
            for w in weights:
                for stage in range(3):
                    give(w, step - 7, stage).wait_send()
                for half in range(2):
                    give_twin(w, step - 7, half).wait_send()

    for k in range(1, 16):
        tell(k).wait_send()


def hand_over(w_from, state, w_to, m_to, v_to, m_by, v_by, sem):
    inward = [pltpu.make_async_copy(state.at[0], m_by, sem.at[0]), pltpu.make_async_copy(state.at[1], v_by, sem.at[1])]
    outward = [pltpu.make_async_copy(m_by, m_to, sem.at[0]), pltpu.make_async_copy(v_by, v_to, sem.at[1])]
    cuts = [(layer, x) for layer in range(LAYERS) for x in range(2)]
    weight = [pltpu.make_async_copy(w_from.at[cut], w_to.at[cut], sem.at[2 + n]) for n, cut in enumerate(cuts)]
    for copy in inward + weight:
        copy.start()
    for copy, back in zip(inward, outward):
        copy.wait()
        back.start()
    for copy in outward + weight:
        copy.wait()


def solution(mesh):
    def step(*arrays):
        terms, whole, m, v = (arrays[i : i + 3] for i in (0, 3, 6, 9))
        weights = [Weight(k, *one.shape[1:]) for k, one in enumerate(m)]
        count = 16 * sum(one.size for one in m)
        cut = [(LAYERS, 2, 2, 2, 2, w.rows, w.columns) for w in weights]
        held = lambda n, extra=(), dtype=BF16: [pltpu.VMEM((n, *extra, *w.shape), dtype) for w in weights]
        scratch = (
            held(HELD, (2, 2))
            + held(HELD, (2,))
            + held(HELD)
            + held(RING)
            + held(RING, dtype=F32)
            + held(RING, dtype=F32)
            + [pltpu.VMEM((8, w.shape[1]), F32) for w in weights]
            + [pltpu.VMEM((8, 128), F32), pltpu.VMEM((15, 8, 128), F32)]
            + [pltpu.SemaphoreType.DMA((SLOTS, 3))] * 3
            + [pltpu.SemaphoreType.DMA((SLOTS, 3, 3))] * 4
            + [pltpu.SemaphoreType.DMA((SLOTS, 2, 3))] * 2
            + [pltpu.SemaphoreType.DMA((RING, 5, 3))]
            + [pltpu.SemaphoreType.DMA((15,))] * 2
        )
        anywhere = pl.BlockSpec(memory_space=pl.ANY)
        out = pl.pallas_call(
            lambda *refs: kernel(weights, float(count), *refs),
            out_shape=[pltpu.VMEM(c, BF16) for c in cut] + [jax.ShapeDtypeStruct((ROOM, *one.shape), F32) for one in m],
            in_specs=[anywhere] * 12,
            out_specs=[pl.BlockSpec(memory_space=pltpu.VMEM)] * 3 + [anywhere] * 3,
            scratch_shapes=scratch,
            compiler_params=pltpu.CompilerParams(collective_id=0, has_side_effects=True, vmem_limit_bytes=GRANT),
            name="step",
        )(*(t.reshape(c) for t, c in zip(terms, cut)), *(t.reshape(c) for t, c in zip(whole, cut)), *m, *v)
        new = [
            pl.pallas_call(
                hand_over,
                out_shape=[jax.ShapeDtypeStruct(cut[w.k], BF16)] + [jax.ShapeDtypeStruct(m[w.k].shape, F32)] * 2,
                in_specs=[pl.BlockSpec(memory_space=pltpu.VMEM), anywhere],
                out_specs=[anywhere] * 3,
                scratch_shapes=[pltpu.VMEM(m[w.k].shape, F32)] * 2 + [pltpu.SemaphoreType.DMA((6,))],
                compiler_params=pltpu.CompilerParams(vmem_limit_bytes=5 * 2**20),
                name="hand_over",
            )(*out[w.k :: 3])
            for w in weights
        ]
        return (*(one[0].reshape(t.shape) for one, t in zip(new, whole)), *(one[1] for one in new), *(one[2] for one in new))

    all_of, cut = P(None, None, None), P(None, "dp", None)
    return jax.shard_map(
        step,
        mesh=mesh,
        in_specs=(P(("rep", "dp"), None, None, None),) * 3 + (all_of,) * 3 + (cut,) * 6,
        out_specs=(P("rep", None, None),) * 3 + (P("rep", "dp", None),) * 6,
        check_vma=False,
    )
```

time: 420 us -> 396 us (0.943)
  local copies, waits for them, and re-layouts: 51 us -> 0 us
  Pallas kernels: 368 us -> 395 us
    unnamed x33 -> x0, local copies, waits for them, and re-layouts: 51 us -> none
    pallas_call x0 -> x3, Pallas kernels: none -> 26.3 us  [step(): pl.pallas_call(hand_over, out_shape=[jax.ShapeDtypeStruct(cut[w.k], BF16)...]
where the time goes in v2:
time: 396 us; the launch traced here: 395 us
  Pallas kernels  395 us (100%)
    pallas_call x1, Pallas kernels, step(): pl.pallas_call(lambda *refs: kernel(weights, float(count), *refs), out_sh...  368 us
    pallas_call x3, Pallas kernels, step(): pl.pallas_call(hand_over, out_shape=[jax.ShapeDtypeStruct(cut[w.k], BF16)...  26.3 us

profile of v2, /device:TPU:0, one launch (start us, length us, event | category | flops | bytes accessed | tf_op | source)
XLA Modules:
  0.0 395.4 jit_solution(16893806569283558779)
XLA Ops:
  0.6 368.4 %step.1 = (bf16[2,2,2,2,2,80,3584]{6,5,4,3,2,1,0:T(8,128)(2,1)S(1)}, bf16[2,2,2,2,2,80,3584]{6,5,4,3,2,1,0:T(8,128)(2,1)S(1)}, bf16[2,2,2,2,2,224,1280]{6,5,4,3,...) custom-call(bf16[2,2,2,2,2,80,3584]{6,5,4,3,2,1,0:T(8,128)(2,1)} %bi, ...), custom_call_target="tpu_custom_call" | custom-call | tf_op jit(solution)/shard_map/step/pallas_call | solution.py:352
  369.1 8.8 %hand_over.3 = (bf16[2,2,2,2,2,80,3584]{6,5,4,3,2,1,0:T(8,128)(2,1)}, f32[2,80,3584]{2,1,0:T(8,128)}, f32[2,80,3584]{2,1,0:T(8,128)}) custom-call(bf16[2,2,2,2,2,80,3584]{6,5,4,3,2,1,0:T(8,128)(2,1)S(1)} %get-tuple-element.24.w_from, f32[32,2,80,3584]{3,2,1,0:T(8,128)} %get-tuple-element.25.state), custom_call_target="tpu_custom_call" | custom-call | tf_op jit(solution)/shard_map/hand_over/pallas_call | solution.py:362
  377.9 8.8 %hand_over.4 = (bf16[2,2,2,2,2,80,3584]{6,5,4,3,2,1,0:T(8,128)(2,1)}, f32[2,80,3584]{2,1,0:T(8,128)}, f32[2,80,3584]{2,1,0:T(8,128)}) custom-call(bf16[2,2,2,2,2,80,3584]{6,5,4,3,2,1,0:T(8,128)(2,1)S(1)} %get-tuple-element.27.w_from, f32[32,2,80,3584]{3,2,1,0:T(8,128)} %get-tuple-element.28.state), custom_call_target="tpu_custom_call" | custom-call | tf_op jit(solution)/shard_map/hand_over/pallas_call | solution.py:362
  386.7 8.8 %hand_over.5 = (bf16[2,2,2,2,2,224,1280]{6,5,4,3,2,1,0:T(8,128)(2,1)}, f32[2,224,1280]{2,1,0:T(8,128)}, f32[2,224,1280]{2,1,0:T(8,128)}) custom-call(bf16[2,2,2,2,2,224,1280]{6,5,4,3,2,1,0:T(8,128)(2,1)S(1)} %get-tuple-element.30.w_from, f32[32,2,224,1280]{3,2,1,0:T(8,128)} %get-tuple-element.31.state), custom_call_target="tpu_custom_call" | custom-call | tf_op jit(solution)/shard_map/hand_over/pallas_call | solution.py:362

commit v3 on v2

--- a/solution.py
+++ b/solution.py
@@ -12,9 +12,10 @@
 WAVES = LAYERS * PARTS
 SLOTS = 8
 HELD = 6
-RING = 4
+RING = 6
 ROOM = 32
-GRANT = 8 * 2**20
+GRANT = 9 * 2**20
+LEAD = 3
 AHEAD = 3
 ORDERS = ((0, 1, 2), (1, 2, 0), (2, 0, 1))
 BITS = (8, 4, 2)
@@ -154,11 +155,6 @@
     for wave in range(AHEAD):
         for w in weights:
             swap(w, wave).start()
-    for wave in range(RING):
-        for w in weights:
-            for copy in fetch(w, wave):
-                copy.start()
-
     def drain(wave):
         for w in weights:
             swap(w, wave).wait_send()
@@ -167,6 +163,10 @@
 
     @pl.loop(0, WAVES + 3)
     def _(step):
+        @pl.when(step >= 4)
+        def _():
+            drain(step - 4)
+
         @pl.when(step < WAVES)
         def _():
             for w in weights:
@@ -176,15 +176,15 @@
 
         @pl.when(step + AHEAD < WAVES)
         def _():
-            wave = step + AHEAD
-
-            @pl.when(wave >= SLOTS)
-            def _():
-                drain(wave - SLOTS)
-
-            for w in weights:
-                load(w, wave).start()
-                swap(w, wave).start()
+            for w in weights:
+                load(w, step + AHEAD).start()
+                swap(w, step + AHEAD).start()
+
+        @pl.when((step >= SLOTS) & (step < SLOTS + RING))
+        def _():
+            for w in weights:
+                for copy in fetch(w, step - SLOTS):
+                    copy.start()
 
         for stage in (1, 2):
 
@@ -200,9 +200,7 @@
                 pass_on(w, step - 3, 2).wait_recv()
                 finish(w, step - 3)
 
-    @pl.loop(WAVES - SLOTS, WAVES)
-    def _(wave):
-        drain(wave)
+    drain(WAVES - 1)
 
     mine = jnp.zeros((8, 128), F32)
     for w in weights:
@@ -251,62 +249,70 @@
         ref = out_at(w, wave, {axis: side}, core)
         return remote(ref, ref, back_send.at[slot, half, w.k], back_recv.at[slot, half, w.k], twin)
 
-    @pl.loop(0, WAVES + 7)
+    def begin(wave):
+        for w in weights:
+            for copy in fetch(w, wave):
+                copy.wait()
+            update(w, wave)
+            give(w, wave, 0).start()
+        for w in weights:
+            for copy in put(w, wave):
+                copy.start()
+
+    @pl.loop(0, LEAD)
+    def _(wave):
+        begin(wave)
+
+    @pl.loop(0, WAVES + 5)
     def _(step):
+        @pl.when(step >= 5)
+        def _():
+            for w in weights:
+                for stage in range(3):
+                    give(w, step - 5, stage).wait_send()
+                for half in range(2):
+                    give_twin(w, step - 5, half).wait_send()
+
+        @pl.when(step + LEAD < WAVES)
+        def _():
+            begin(step + LEAD)
+
         @pl.when(step < WAVES)
         def _():
             for w in weights:
-                for copy in fetch(w, step):
+                give(w, step, 0).wait_recv()
+                give(w, step, 1).start()
+
+        @pl.when((step >= 1) & (step - 1 < WAVES))
+        def _():
+            for w in weights:
+                give(w, step - 1, 1).wait_recv()
+                give(w, step - 1, 2).start()
+                give_twin(w, step - 1, 0).start()
+
+        @pl.when((step >= 2) & (step - 2 < WAVES))
+        def _():
+            for w in weights:
+                give(w, step - 2, 2).wait_recv()
+                give_twin(w, step - 2, 1).start()
+
+        @pl.when(step < WAVES)
+        def _():
+            for w in weights:
+                for copy in put(w, step):
                     copy.wait()
-                update(w, step)
-                give(w, step, 0).start()
-                for copy in put(w, step):
+
+        @pl.when(step + RING < WAVES)
+        def _():
+            for w in weights:
+                for copy in fetch(w, step + RING):
                     copy.start()
 
-        @pl.when((step >= 1) & (step - 1 < WAVES))
-        def _():
-            for w in weights:
-                give(w, step - 1, 0).wait_recv()
-                give(w, step - 1, 1).start()
-
-        @pl.when((step >= 2) & (step - 2 < WAVES))
-        def _():
-            for w in weights:
-                give(w, step - 2, 1).wait_recv()
-                give(w, step - 2, 2).start()
-                give_twin(w, step - 2, 0).start()
-
-        @pl.when((step >= 3) & (step - 3 < WAVES))
-        def _():
-            for w in weights:
-                give(w, step - 3, 2).wait_recv()
-                give_twin(w, step - 3, 1).start()
-
-        @pl.when((step >= 2) & (step - 2 < WAVES))
-        def _():
-            for w in weights:
-                for copy in put(w, step - 2):
-                    copy.wait()
-
-        @pl.when((step >= 2) & (step + 2 < WAVES))
-        def _():
-            for w in weights:
-                for copy in fetch(w, step + 2):
-                    copy.start()
-
-        @pl.when((step >= 5) & (step - 5 < WAVES))
+        @pl.when((step >= 4) & (step - 4 < WAVES))
         def _():
             for w in weights:
                 for half in range(2):
-                    give_twin(w, step - 5, half).wait_recv()
-
-        @pl.when((step >= 7) & (step - 7 < WAVES))
-        def _():
-            for w in weights:
-                for stage in range(3):
-                    give(w, step - 7, stage).wait_send()
-                for half in range(2):
-                    give_twin(w, step - 7, half).wait_send()
+                    give_twin(w, step - 4, half).wait_recv()
 
     for k in range(1, 16):
         tell(k).wait_send()

time: 396 us -> 395 us (level)
  no operation moved by 1% of the time
where the time goes in v3:
time: 395 us
  Pallas kernels  394 us (100%)
    pallas_call x1, Pallas kernels, step(): pl.pallas_call(lambda *refs: kernel(weights, float(count), *refs), out_sh...  368 us
    pallas_call x3, Pallas kernels, step(): pl.pallas_call(hand_over, out_shape=[jax.ShapeDtypeStruct(cut[w.k], BF16)...  26.3 us

profile of v3, /device:TPU:0, one launch (start us, length us, event | category | flops | bytes accessed | tf_op | source)
XLA Modules:
  0.0 395.0 jit_solution(15117501776261940378)
XLA Ops:
  0.6 368.0 %step.1 = (bf16[2,2,2,2,2,80,3584]{6,5,4,3,2,1,0:T(8,128)(2,1)S(1)}, bf16[2,2,2,2,2,80,3584]{6,5,4,3,2,1,0:T(8,128)(2,1)S(1)}, bf16[2,2,2,2,2,224,1280]{6,5,4,3,...) custom-call(bf16[2,2,2,2,2,80,3584]{6,5,4,3,2,1,0:T(8,128)(2,1)} %bi, ...), custom_call_target="tpu_custom_call" | custom-call | tf_op jit(solution)/shard_map/step/pallas_call | solution.py:358
  368.6 8.8 %hand_over.3 = (bf16[2,2,2,2,2,80,3584]{6,5,4,3,2,1,0:T(8,128)(2,1)}, f32[2,80,3584]{2,1,0:T(8,128)}, f32[2,80,3584]{2,1,0:T(8,128)}) custom-call(bf16[2,2,2,2,2,80,3584]{6,5,4,3,2,1,0:T(8,128)(2,1)S(1)} %get-tuple-element.24.w_from, f32[32,2,80,3584]{3,2,1,0:T(8,128)} %get-tuple-element.25.state), custom_call_target="tpu_custom_call" | custom-call | tf_op jit(solution)/shard_map/hand_over/pallas_call | solution.py:368
  377.4 8.8 %hand_over.4 = (bf16[2,2,2,2,2,80,3584]{6,5,4,3,2,1,0:T(8,128)(2,1)}, f32[2,80,3584]{2,1,0:T(8,128)}, f32[2,80,3584]{2,1,0:T(8,128)}) custom-call(bf16[2,2,2,2,2,80,3584]{6,5,4,3,2,1,0:T(8,128)(2,1)S(1)} %get-tuple-element.27.w_from, f32[32,2,80,3584]{3,2,1,0:T(8,128)} %get-tuple-element.28.state), custom_call_target="tpu_custom_call" | custom-call | tf_op jit(solution)/shard_map/hand_over/pallas_call | solution.py:368
  386.2 8.8 %hand_over.5 = (bf16[2,2,2,2,2,224,1280]{6,5,4,3,2,1,0:T(8,128)(2,1)}, f32[2,224,1280]{2,1,0:T(8,128)}, f32[2,224,1280]{2,1,0:T(8,128)}) custom-call(bf16[2,2,2,2,2,224,1280]{6,5,4,3,2,1,0:T(8,128)(2,1)S(1)} %get-tuple-element.30.w_from, f32[32,2,224,1280]{3,2,1,0:T(8,128)} %get-tuple-element.31.state), custom_call_target="tpu_custom_call" | custom-call | tf_op jit(solution)/shard_map/hand_over/pallas_call | solution.py:368
